TPU v7x, 32 devices: a whole 2x2x4 slice. The times are simulated.
32 devices in a mesh: rep: 2 (over x), zero: 16 (over z, y, core).
Axes of the slice: x: 2, y: 2, z: 4, core: 2. Of those that a mesh axis runs over, the one named last changes fastest.
Arguments:
- acts: bfloat16 [256, 8192], P('rep', 'zero'), may hold values from -6 to 6
- grads_out: bfloat16 [256, 8192], P('rep', 'zero'), may hold values from -12 to 12
- act_inverse: bfloat16 [8192, 8192], P('zero'), as said below
- grad_inverse: bfloat16 [8192, 8192], P('zero'), as said below
Outputs:
- precond: float32 [8192, 8192], P('zero')
Inputs may be any that keep to these rules, and one draw needn't show every extreme that they name: act_inverse is symmetric. grad_inverse is symmetric.
All inputs are finite; a program needn't handle non-finite values.
Results may differ from a plain program's by a relative error of at most 0.004.
Values may be sent and summed in bfloat16 or wider, within the bound.
A program may use at most 128 MiB of HBM per device.

v0:
```python
import jax
import jax.numpy as jnp
from jax import lax
from jax.sharding import PartitionSpec as P


def on_device(acts, grads_out, act_inverse, grad_inverse):
    tok_group = acts.shape[0]
    total_tokens = tok_group * lax.axis_size("rep")
    term = jnp.dot(acts, act_inverse, preferred_element_type=jnp.float32)
    act_pre = lax.psum(term, "zero").astype(jnp.bfloat16)
    grad_pre_t = lax.dot_general(
        grad_inverse,
        lax.all_gather(grads_out, "zero", axis=1, tiled=True),
        (((1,), (1,)), ((), ())),
        preferred_element_type=jnp.float32,
    ).astype(jnp.bfloat16)
    partial_rows = jnp.dot(grad_pre_t, act_pre, preferred_element_type=jnp.float32) / jnp.float32(
        total_tokens
    )
    return lax.psum(partial_rows, "rep")


def solution(mesh):
    return jax.shard_map(
        on_device,
        mesh=mesh,
        in_specs=(P("rep", "zero"), P("rep", "zero"), P("zero", None), P("zero", None)),
        out_specs=P("zero", None),
        check_vma=False,
    )
```

profile of v0, /device:TPU:0, one launch (start us, length us, event | category | flops | bytes accessed | tf_op | source)
XLA Modules:
  0.0 535.1 jit_solution(13765443983158648855)
XLA Ops:
  6.5 0.0 copy-start
  6.5 0.0 all-gather.2.cloned.1.call-start
  6.5 0.7 all-gather.2.cloned.1.call-update
  7.3 0.0 all-reduce.3.cloned.1.call-start
  7.3 0.1 copy-done
  7.4 6.7 %fusion.1 = f32[128,8192]{1,0:T(8,128)} fusion(bf16[128,512]{1,0:T(8,128)(2,1)S(1)} %copy-done, bf16[512,8192]{1,0:T(8,128)(2,1)} %param.6), kind=kOutput, calls=%fused_computation.3 | convolution fusion | flops 1073741824 | bytes 12713984 | tf_op jit(solution)/shard_map/dot_general | solution.py:10
  14.1 104.8 %all-reduce.4 = bf16[128,8192]{1,0:T(8,128)(2,1)S(1)} all-reduce(f32[128,8192]{1,0:T(8,128)} %fusion.1), channel_id=1, replica_groups=mesh['rep'=2,'zero'=16] {'zero'}, use_global_device_ids=true, to_apply=%region_0.0 | all-reduce | flops 1048576 | bytes 6291456 | tf_op jit(solution)/shard_map/psum | solution.py:11
  118.9 0.0 all-gather.2.cloned.1.call-done
  118.9 19.0 %convolution_multiply_fusion = f32[512,8192]{1,0:T(8,128)} fusion(bf16[128,8192]{1,0:T(8,128)(2,1)S(1)} %all-reduce.4, bf16[512,8192]{1,0:T(8,128)(2,1)} %param.7, bf16[128,8192]{1,0:T(8,128)(2,1)} %all-gather.2.cloned.1.call-done), kind=kOutput, calls=%fused_computation | convolution fusion | flops 2151743488 | bytes 29360128 | tf_op jit(solution)/shard_map/dot_general | solution.py:18
  137.9 0.0 all-reduce.3.cloned.1.call-update
  137.9 378.7 %all-reduce.3.cloned.1.call-done = f32[512,8192]{1,0:T(8,128)} async-done(((f32[512,8192]{1,0:T(8,128)}), f32[512,8192]{1,0:T(8,128)}) %all-reduce.3.cloned.1.call-update) | async-done | bytes 16777232 | tf_op jit(solution)/shard_map/psum | solution.py:21
  516.6 0.0 copy-start.1
  516.6 11.7 %copy.8 = f32[512,8192]{1,0:T(8,128)} copy(f32[512,8192]{1,0:T(8,128)} %all-reduce.3.cloned.1.call-done) | data formatting | bytes 33554432
  528.3 0.0 copy-done.1
Async XLA Ops:
  6.5 0.9 copy-start
  6.5 112.4 %all-gather.2.cloned.1.call-start = ((), (), s32[]{:S(2)}) async-start(), calls=%async_computation | async-start | bytes 2228224 | tf_op jit(solution)/shard_map/all_gather | solution.py:14
  7.3 509.3 %all-reduce.3.cloned.1.call-start = ((), (), s32[]{:S(2)}) async-start(), calls=%async_computation.1 | async-start | bytes 33554432 | tf_op jit(solution)/shard_map/psum | solution.py:21
  516.6 11.7 %copy-start.1 = (bf16[128,512]{1,0:T(8,128)(2,1)S(1)}, bf16[128,512]{1,0:T(8,128)(2,1)}, u32[]{:S(2)}) copy-start(bf16[128,512]{1,0:T(8,128)(2,1)} %param.4) | copy-start | bytes 393220
Sparse Core Ops, SparseCore 0:
  9.5 56.5 all-gather.1
  138.1 378.5 all-reduce.2
where the time goes:
time: 535 us
  waiting for transfers between devices  379 us (71%)
  blocking collectives  105 us (20%)
  matrix products  25.6 us (5%)
  between operations  13.4 us (3%)
  local copies, waits for them, and re-layouts  11.8 us (2%)
    psum x1, waiting for transfers between devices, on_device(): return lax.psum(partial_rows, 'rep')  379 us
    psum x1, blocking collectives, on_device(): act_pre = lax.psum(term, 'zero').astype(jnp.bfloat16)  105 us
    dot_general x1, matrix products, on_device(): jnp.dot(grad_pre_t, act_pre, preferred_element_type=jnp.float32)  19 us
    unnamed x5, local copies, waits for them, and re-layouts  11.8 us
  transfers between devices with their start and end apart: 2, of which 1 were waited for; matrix products, arithmetic and copies ran while one was open for 1% of the time, Pallas kernels for 0%

commit v1 on v0

--- a/solution.py
+++ b/solution.py
@@ -18,7 +18,7 @@
     partial_rows = jnp.dot(grad_pre_t, act_pre, preferred_element_type=jnp.float32) / jnp.float32(
         total_tokens
     )
-    return lax.psum(partial_rows, "rep")
+    return jnp.sum(lax.all_gather(partial_rows, "rep"), axis=0)
 
 
 def solution(mesh):

time: 535 us -> 554 us (1.036)
  other arithmetic: 0 us -> 19.5 us
  local copies, waits for them, and re-layouts: 11.8 us -> 0.14 us
  waiting for transfers between devices: 379 us -> 390 us
    all_gather x0 -> x1, waiting for transfers between devices: none -> 389 us  [on_device(): return jnp.sum(lax.all_gather(partial_rows, 'rep'), axis=0)]
    psum x1 -> x0, waiting for transfers between devices: 379 us -> none  [on_device(): return lax.psum(partial_rows, 'rep')]
    reduce_sum x0 -> x1, other arithmetic: none -> 19.5 us  [on_device(): return jnp.sum(lax.all_gather(partial_rows, 'rep'), axis=0)]
    unnamed x5 -> x4, local copies, waits for them, and re-layouts: 11.8 us -> 0.14 us
where the time goes in v1:
time: 554 us; the launch traced here: 553 us
  waiting for transfers between devices  390 us (70%)
  blocking collectives  105 us (19%)
  matrix products  25.6 us (5%)
  other arithmetic  19.5 us (4%)
  between operations  13.4 us (2%)
    all_gather x1, waiting for transfers between devices, on_device(): return jnp.sum(lax.all_gather(partial_rows, 'rep'), axis=0)  389 us
    psum x1, blocking collectives, on_device(): act_pre = lax.psum(term, 'zero').astype(jnp.bfloat16)  105 us
    reduce_sum x1, other arithmetic, on_device(): return jnp.sum(lax.all_gather(partial_rows, 'rep'), axis=0)  19.5 us
    dot_general x1, matrix products, on_device(): jnp.dot(grad_pre_t, act_pre, preferred_element_type=jnp.float32)  19 us
  transfers between devices with their start and end apart: 2, of which 1 were waited for; matrix products, arithmetic and copies ran while one was open for 1% of the time, Pallas kernels for 0%

profile of v1, /device:TPU:0, one launch (start us, length us, event | category | flops | bytes accessed | tf_op | source)
XLA Modules:
  0.0 553.5 jit_solution(2958811321300158330)
XLA Ops:
  6.5 0.0 copy-start
  6.5 0.0 all-gather.4.cloned.1.call-start
  6.5 0.7 all-gather.4.cloned.1.call-update
  7.3 0.0 all-gather.6.cloned.1.call-start
  7.3 0.1 copy-done
  7.4 6.7 %fusion.1 = f32[128,8192]{1,0:T(8,128)} fusion(bf16[128,512]{1,0:T(8,128)(2,1)S(1)} %copy-done, bf16[512,8192]{1,0:T(8,128)(2,1)} %param.6), kind=kOutput, calls=%fused_computation.3 | convolution fusion | flops 1073741824 | bytes 12713984 | tf_op jit(solution)/shard_map/dot_general | solution.py:10
  14.1 104.8 %all-reduce.1 = bf16[128,8192]{1,0:T(8,128)(2,1)S(1)} all-reduce(f32[128,8192]{1,0:T(8,128)} %fusion.1), channel_id=1, replica_groups=mesh['rep'=2,'zero'=16] {'zero'}, use_global_device_ids=true, to_apply=%region_0.0 | all-reduce | flops 1048576 | bytes 6291456 | tf_op jit(solution)/shard_map/psum | solution.py:11
  118.9 0.0 all-gather.4.cloned.1.call-done
  118.9 19.0 %convolution_multiply_fusion = f32[512,8192]{1,0:T(8,128)} fusion(bf16[128,8192]{1,0:T(8,128)(2,1)S(1)} %all-reduce.1, bf16[512,8192]{1,0:T(8,128)(2,1)} %param.7, bf16[128,8192]{1,0:T(8,128)(2,1)} %all-gather.4.cloned.1.call-done), kind=kOutput, calls=%fused_computation | convolution fusion | flops 2151743488 | bytes 29360128 | tf_op jit(solution)/shard_map/dot_general | solution.py:18
  137.9 0.0 all-gather.6.cloned.1.call-update
  137.9 389.2 %all-gather.6.cloned.1.call-done = f32[1024,8192]{1,0:T(8,128)} async-done(((f32[512,8192]{1,0:T(8,128)}), f32[1024,8192]{1,0:T(8,128)}) %all-gather.6.cloned.1.call-update) | async-done | bytes 33554448 | tf_op jit(solution)/shard_map/all_gather | solution.py:21
  527.1 0.0 copy-start.1
  527.1 19.5 %reduce_sum.9 = f32[512,8192]{1,0:T(8,128)} reduce(f32[2,512,8192]{2,1,0:T(8,128)} %bitcast.6, f32[]{:T(128)} %constant.4.clone.1), dimensions={0}, to_apply=%region_1.0 | reduce | flops 4194304 | bytes 50331652 | tf_op jit(solution)/shard_map/reduce_sum | solution.py:21
  546.6 0.0 copy-done.1
Async XLA Ops:
  6.5 0.9 copy-start
  6.5 112.4 %all-gather.4.cloned.1.call-start = ((), (), s32[]{:S(2)}) async-start(), calls=%async_computation | async-start | bytes 2228224 | tf_op jit(solution)/shard_map/all_gather | solution.py:14
  7.3 519.9 %all-gather.6.cloned.1.call-start = ((), (), s32[]{:S(2)}) async-start(), calls=%async_computation.1 | async-start | bytes 50331648 | tf_op jit(solution)/shard_map/all_gather | solution.py:21
  527.1 19.5 %copy-start.1 = (bf16[128,512]{1,0:T(8,128)(2,1)S(1)}, bf16[128,512]{1,0:T(8,128)(2,1)}, u32[]{:S(2)}) copy-start(bf16[128,512]{1,0:T(8,128)(2,1)} %param.4) | copy-start | bytes 393220
Sparse Core Ops, SparseCore 0:
  9.5 56.5 all-gather.3
  138.1 389.0 all-gather.5
